TPU v7x, 32 devices: a whole 2x2x4 slice. The times are simulated.
32 devices in a mesh: rep: 2 (over x), ep: 4 (over z), fsdp: 4 (over y, core).
Axes of the slice: x: 2, y: 2, z: 4, core: 2. Of those that a mesh axis runs over, the one named last changes fastest.
Arguments:
- x_in: bfloat16 [8192, 4096], P(('rep', 'ep', 'fsdp')), parts along dimension 0
- norm_w: float32 [2, 4096], replicated
- router_w: bfloat16 [2, 4096, 8], replicated
- gate_w: bfloat16 [2, 8, 4096, 1376], P(None, 'ep', None, 'fsdp')
- up_w: bfloat16 [2, 8, 4096, 1376], P(None, 'ep', None, 'fsdp')
- down_w: bfloat16 [2, 8, 1376, 4096], P(None, 'ep', 'fsdp')
- routes: int32 [2, 8192, 2], P(None, ('rep', 'ep', 'fsdp')), parts along dimension 1
Outputs:
- output: bfloat16 [8192, 4096], P(('rep', 'ep', 'fsdp')), parts along dimension 0
There are 2 independent parts. A program takes and returns all parts, laid end to end along the dimension named above; an argument that names none is the same for every part.
All inputs are finite; a program needn't handle non-finite values.
Results may differ from a plain program's by a relative error of at most 0.0123691.
Values are sent between devices in bfloat16 or wider.
A program may use at most 1 GiB of HBM per device.

v0:
```python
import jax
import jax.numpy as jnp
from jax import lax
from jax.sharding import PartitionSpec as P

NORM_EPS = 1e-5


def rms_norm(stream, norm_row):
    widened = stream.astype(jnp.float32)
    inv_rms = lax.rsqrt(jnp.mean(widened * widened, axis=-1, keepdims=True) + NORM_EPS)
    return (widened * inv_rms * norm_row).astype(jnp.bfloat16)


def route_gates(hidden, router_l, routes_l):
    logits = jnp.dot(hidden, router_l, preferred_element_type=jnp.float32)
    return jax.nn.softmax(jnp.take_along_axis(logits, routes_l, axis=-1), axis=-1)


def capacity_of(tok_dev, top_k, experts):
    return 8 * ((2 * tok_dev * top_k + 8 * experts - 1) // (8 * experts))


def slot_plan(routes_l, experts, capacity, owners):
    tok_dev, top_k = routes_l.shape
    flat_ids = routes_l.reshape(-1)
    onehot = (flat_ids[:, None] == jnp.arange(experts, dtype=flat_ids.dtype)[None, :]).astype(jnp.int32)
    pair_rank = jnp.sum((jnp.cumsum(onehot, axis=0) - 1) * onehot, axis=1)
    n_local = experts // owners
    pair_slot = ((flat_ids % n_local) * owners + flat_ids // n_local) * capacity + pair_rank
    pair_token = jnp.arange(tok_dev * top_k, dtype=jnp.int32) // top_k
    slot_token = jnp.zeros((experts * capacity,), jnp.int32).at[pair_slot].set(pair_token)
    return pair_slot, slot_token


def expert_ffn(expert_rows, gate_full, up_full, down_full):
    pre_gate = jnp.einsum("erd,edf->erf", expert_rows, gate_full, preferred_element_type=jnp.float32)
    pre_up = jnp.einsum("erd,edf->erf", expert_rows, up_full, preferred_element_type=jnp.float32)
    inner_act = (jax.nn.silu(pre_gate) * pre_up).astype(jnp.bfloat16)
    return jnp.einsum("erf,efd->erd", inner_act, down_full, preferred_element_type=jnp.float32).astype(jnp.bfloat16)


def combine(stream, gate_probs, pair_out):
    mixed_sum = jnp.sum(gate_probs[..., None] * pair_out.astype(jnp.float32), axis=-2)
    return (stream.astype(jnp.float32) + mixed_sum).astype(jnp.bfloat16)


def solution(mesh):
    owners = mesh.shape["ep"]
    token_spec = P(("rep", "ep", "fsdp"), None)
    expert_in_spec = P(None, "ep", None, "fsdp")
    expert_out_spec = P(None, "ep", "fsdp", None)
    route_spec = P(None, ("rep", "ep", "fsdp"), None)

    def device_step(x_in, norm_w, router_w, gate_w, up_w, down_w, routes):
        layers, tok_dev, top_k = routes.shape
        experts = router_w.shape[2]
        n_local = gate_w.shape[1]
        d_model = x_in.shape[1]
        capacity = capacity_of(tok_dev, top_k, experts)
        stream = x_in
        for layer_idx in range(layers):
            routes_l = routes[layer_idx]
            hidden = rms_norm(stream, norm_w[layer_idx])
            gate_probs = route_gates(hidden, router_w[layer_idx], routes_l)
            pair_slot, slot_token = slot_plan(routes_l, experts, capacity, owners)
            send_buf = hidden[slot_token].reshape(n_local, owners, capacity, d_model)
            recv_buf = lax.all_to_all(send_buf, "ep", 1, 1, tiled=True)
            gate_full = lax.all_gather(gate_w[layer_idx], "fsdp", axis=2, tiled=True)
            up_full = lax.all_gather(up_w[layer_idx], "fsdp", axis=2, tiled=True)
            down_full = lax.all_gather(down_w[layer_idx], "fsdp", axis=1, tiled=True)
            expert_out = expert_ffn(recv_buf.reshape(n_local, owners * capacity, d_model), gate_full, up_full, down_full)
            back_buf = lax.all_to_all(expert_out.reshape(n_local, owners, capacity, d_model), "ep", 1, 1, tiled=True)
            pair_out = back_buf.reshape(experts * capacity, d_model)[pair_slot].reshape(tok_dev, top_k, d_model)
            stream = combine(stream, gate_probs, pair_out)
        return stream

    return jax.shard_map(device_step, mesh=mesh,
                         in_specs=(token_spec, P(), P(), expert_in_spec, expert_in_spec, expert_out_spec, route_spec),
                         out_specs=token_spec, check_vma=False)
```

profile of v0, /device:TPU:0, one launch (start us, length us, event | category | flops | bytes accessed | tf_op | source)
XLA Modules:
  0.0 1227.9 jit_solution(12273631702731363420)
XLA Ops:
  6.5 10.4 fusion.62
  17.0 10.4 fusion.61
  27.5 10.3 fusion.60
  38.4 0.5 all-gather.21.cloned.1.call-update
  39.6 1.1 reduce-window.14
  41.1 2.4 scatter_custom_fusion
  44.1 0.6 fusion.63
  44.8 2.2 fusion.20
  47.0 7.6 gather_fusion
  54.6 7.7 copy.13
  62.4 192.8 %all_to_all.20 = bf16[2,4,128,4096]{3,2,0,1:T(8,128)(2,1)} all-to-all(bf16[2,4,128,4096]{3,2,0,1:T(8,128)(2,1)} %copy.13), channel_id=1, replica_groups=mesh['rep'=2,'ep'=4,'fsdp'=4] {'ep'}, dimensions={1} | all-to-all | bytes 16777216 | tf_op jit(solution)/shard_map/all_to_all | solution.py:68
  255.2 7.7 copy.14
  262.9 19.3 %fusion.10 = f32[2,512,1376]{1,2,0:T(8,128)} fusion(bf16[2,512,4096]{2,1,0:T(8,128)(2,1)} %bitcast.102, bf16[1,2,4096,1376]{2,3,1,0:T(8,128)(2,1)} %all-gather.13.cloned.1.call-done), kind=kOutput, calls=%fused_computation.18 | convolution fusion | flops 11542724608 | bytes 36569088 | tf_op jit(solution)/shard_map/erd,edf->erf/dot_general | solution.py:37
  282.2 17.7 %all-gather.15.cloned.1.call-done = bf16[1,2,4096,1376]{2,3,1,0:T(8,128)(2,1)} async-done(((bf16[1,2,4096,344]{2,3,1,0:T(8,128)(2,1)}), bf16[1,2,4096,1376]{2,3,1,0:T(8,128)(2,1)}) %all-gather.15.cloned.1.call-update) | async-done | bytes 22544400 | tf_op jit(solution)/shard_map/all_gather | solution.py:70
  299.9 20.0 %multiply_convert_fusion.1 = bf16[2,512,1376]{1,2,0:T(8,128)(2,1)} fusion(f32[2,512,1376]{1,2,0:T(8,128)} %fusion.10, bf16[2,512,4096]{2,1,0:T(8,128)(2,1)} %bitcast.103, bf16[1,2,4096,1376]{2,3,1,0:T(8,128)(2,1)} %all-gather.15.cloned.1.call-done), kind=kOutput, calls=%fused_computation.31 | convolution fusion | flops 11551178752 | bytes 39387136 | tf_op jit(solution)/shard_map/erd,edf->erf/dot_general | solution.py:38
  319.9 120.8 %all-gather.17.cloned.1.call-done = bf16[1,2,1376,4096]{3,2,1,0:T(8,128)(2,1)} async-done(((bf16[1,2,344,4096]{3,2,1,0:T(8,128)(2,1)}), bf16[1,2,1376,4096]{3,2,1,0:T(8,128)(2,1)}) %all-gather.17.cloned.1.call-update) | async-done | bytes 22544400 | tf_op jit(solution)/shard_map/all_gather | solution.py:71
  440.8 21.0 %fusion.12 = bf16[2,512,4096]{2,1,0:T(8,128)(2,1)} fusion(bf16[2,512,1376]{1,2,0:T(8,128)(2,1)} %multiply_convert_fusion.1, bf16[1,2,1376,4096]{3,2,1,0:T(8,128)(2,1)} %all-gather.17.cloned.1.call-done), kind=kOutput, calls=%fused_computation.22 | convolution fusion | flops 11546918912 | bytes 33751040 | tf_op jit(solution)/shard_map/erf,efd->erd/dot_general | solution.py:40
  461.8 7.8 copy.15
  469.6 5.7 all-to-all-start.1
  476.6 0.6 fusion.36
  477.3 3.5 gather_fusion.4
  480.9 1.1 reduce-window.16
  482.5 2.8 scatter_custom_fusion.1
  485.8 172.8 %all-to-all-done.1 = bf16[2,4,128,4096]{3,2,0,1:T(8,128)(2,1)} async-done(((bf16[2,4,128,4096]{3,2,0,1:T(8,128)(2,1)}), bf16[2,4,128,4096]{3,2,0,1:T(8,128)(2,1)}, u32[]{:S(2)}, u32[]{:S(2)}) %all-to-all-start.1) | async-done | bytes 8388640 | tf_op jit(solution)/shard_map/all_to_all | solution.py:73
  658.6 7.8 copy.16
  666.4 13.1 %gather_fusion.1 = bf16[512,4096]{1,0:T(8,128)(2,1)} fusion(bf16[1024,4096]{1,0:T(8,128)(2,1)} %bitcast.98, s32[1024]{0:T(1024)S(1)} %pad_clamp_fusion.1), kind=kCustom, calls=%fused_computation.3 | custom fusion | bytes 8390656 | tf_op jit(solution)/shard_map/gather | solution.py:74
  679.5 9.7 reshape.349
  689.2 13.6 %multiply_reduce_fusion.1 = f32[256,4096]{1,0:T(8,128)S(1)} fusion(f32[256,2,4096]{2,1,0:T(2,128)} %reshape.349, f32[256,2]{1,0:T(8,128)S(1)} %fusion.30), kind=kLoop, calls=%fused_computation.21 | loop fusion | flops 3145728 | bytes 12584960 | tf_op jit(solution)/shard_map/reduce_sum | solution.py:44
  702.8 0.8 fusion.22
  703.6 1.3 copy-done.2
  704.9 0.6 fusion.24
  705.6 7.8 gather_fusion.2
  713.4 7.7 copy.18
  721.1 190.1 %all_to_all.21 = bf16[2,4,128,4096]{3,2,0,1:T(8,128)(2,1)} all-to-all(bf16[2,4,128,4096]{3,2,0,1:T(8,128)(2,1)} %copy.18), channel_id=1, replica_groups=mesh['rep'=2,'ep'=4,'fsdp'=4] {'ep'}, dimensions={1} | all-to-all | bytes 16777216 | tf_op jit(solution)/shard_map/all_to_all | solution.py:68
  911.2 7.7 copy.19
  918.9 19.2 %fusion.4 = f32[2,512,1376]{1,2,0:T(8,128)} fusion(bf16[2,512,4096]{2,1,0:T(8,128)(2,1)} %bitcast.104, bf16[1,2,4096,1376]{2,3,1,0:T(8,128)(2,1)} %all-gather.19.cloned.1.call-done), kind=kOutput, calls=%fused_computation.12 | convolution fusion | flops 11542724608 | bytes 36569088 | tf_op jit(solution)/shard_map/erd,edf->erf/dot_general | solution.py:37
  938.2 20.0 %multiply_convert_fusion = bf16[2,512,1376]{1,2,0:T(8,128)(2,1)} fusion(f32[2,512,1376]{1,2,0:T(8,128)} %fusion.4, bf16[2,512,4096]{2,1,0:T(8,128)(2,1)} %bitcast.105, bf16[1,2,4096,1376]{2,3,1,0:T(8,128)(2,1)} %all-gather.21.cloned.1.call-done), kind=kOutput, calls=%fused_computation.30 | convolution fusion | flops 11551178752 | bytes 39387136 | tf_op jit(solution)/shard_map/erd,edf->erf/dot_general | solution.py:38
  958.2 20.9 %fusion.15 = bf16[2,512,4096]{2,1,0:T(8,128)(2,1)} fusion(bf16[2,512,1376]{1,2,0:T(8,128)(2,1)} %multiply_convert_fusion, bf16[1,2,1376,4096]{3,2,1,0:T(8,128)(2,1)} %all-gather.23.cloned.1.call-done), kind=kOutput, calls=%fused_computation.23 | convolution fusion | flops 11546918912 | bytes 33751040 | tf_op jit(solution)/shard_map/erf,efd->erd/dot_general | solution.py:40
  979.0 7.7 copy.20
  986.7 6.1 all-to-all-start.3
  993.1 0.6 fusion.34
  993.7 3.5 gather_fusion.5
  997.8 176.8 %all-to-all-done.3 = bf16[2,4,128,4096]{3,2,0,1:T(8,128)(2,1)} async-done(((bf16[2,4,128,4096]{3,2,0,1:T(8,128)(2,1)}), bf16[2,4,128,4096]{3,2,0,1:T(8,128)(2,1)}, u32[]{:S(2)}, u32[]{:S(2)}) %all-to-all-start.3) | async-done | bytes 8388640 | tf_op jit(solution)/shard_map/all_to_all | solution.py:73
  1174.6 7.7 copy.21
  1182.3 13.0 %gather_fusion.3 = bf16[512,4096]{1,0:T(8,128)(2,1)} fusion(bf16[1024,4096]{1,0:T(8,128)(2,1)} %bitcast.99, s32[1024]{0:T(1024)S(1)} %pad_clamp_fusion), kind=kCustom, calls=%fused_computation.5 | custom fusion | bytes 8390656 | tf_op jit(solution)/shard_map/gather | solution.py:74
  1195.3 9.6 reshape.350
  1205.0 13.6 %multiply_reduce_fusion = f32[256,4096]{1,0:T(8,128)S(1)} fusion(f32[256,2,4096]{2,1,0:T(2,128)} %reshape.350, f32[256,2]{1,0:T(8,128)S(1)} %fusion.32), kind=kLoop, calls=%fused_computation.20 | loop fusion | flops 3145728 | bytes 12584960 | tf_op jit(solution)/shard_map/reduce_sum | solution.py:44
  1218.6 2.0 fusion.25
  (83 shorter events, 5.3 us)
Async XLA Ops:
  6.5 256.3 %all-gather.13.cloned.1.call-start = ((), (), s32[]{:S(2)}) async-start(), calls=%async_computation.4 | async-start | bytes 28180480 | tf_op jit(solution)/shard_map/all_gather | solution.py:69
  16.9 283.0 %all-gather.15.cloned.1.call-start = ((), (), s32[]{:S(2)}) async-start(), calls=%async_computation.5 | async-start | bytes 28180480 | tf_op jit(solution)/shard_map/all_gather | solution.py:70
  27.5 413.3 %all-gather.17.cloned.1.call-start = ((), (), s32[]{:S(2)}) async-start(), calls=%async_computation.6 | async-start | bytes 28180480 | tf_op jit(solution)/shard_map/all_gather | solution.py:71
  37.8 881.1 %all-gather.19.cloned.1.call-start = ((), (), s32[]{:S(2)}) async-start(), calls=%async_computation.7 | async-start | bytes 28180480 | tf_op jit(solution)/shard_map/all_gather | solution.py:69
  37.9 1.1 copy-start.12
  37.9 5.7 copy-start
  37.9 6.2 copy-start.9
  38.4 899.8 %all-gather.21.cloned.1.call-start = ((), (), s32[]{:S(2)}) async-start(), calls=%async_computation.8 | async-start | bytes 28180480 | tf_op jit(solution)/shard_map/all_gather | solution.py:70
  41.0 13.6 %copy-start.13 = (s32[512]{0:T(512)}, s32[512]{0:T(512)S(1)}, u32[]{:S(2)}) copy-start(s32[512]{0:T(512)S(1)} %add_select_fusion) | copy-start | bytes 6148
  41.1 3.0 copy-start.10
  469.6 189.0 %all-to-all-start.1 = ((bf16[2,4,128,4096]{3,2,0,1:T(8,128)(2,1)}), bf16[2,4,128,4096]{3,2,0,1:T(8,128)(2,1)}, u32[]{:S(2)}, u32[]{:S(2)}) async-start(bf16[2,4,128,4096]{3,2,0,1:T(8,128)(2,1)} %copy.15), calls=%async_computation.1 | async-start | bytes 16777216 | tf_op jit(solution)/shard_map/all_to_all | solution.py:73
  475.2 1.4 copy-start.6
  475.3 482.9 %all-gather.23.cloned.1.call-start = ((), (), s32[]{:S(2)}) async-start(), calls=%async_computation.9 | async-start | bytes 28180480 | tf_op jit(solution)/shard_map/all_gather | solution.py:71
  476.0 4.8 copy-start.4
  477.3 8.0 copy-start.11
  689.2 13.6 %copy-start.1 = (bf16[256,4096]{1,0:T(8,128)(2,1)S(1)}, bf16[256,4096]{1,0:T(8,128)(2,1)}, u32[]{:S(2)}) copy-start(bf16[256,4096]{1,0:T(8,128)(2,1)} %param.9) | copy-start | bytes 6291460
  702.8 2.2 copy-start.8
  703.6 1.3 copy-start.2
  986.7 6.1 copy-start.5
  986.7 6.3 copy-start.7
  986.7 187.9 %all-to-all-start.3 = ((bf16[2,4,128,4096]{3,2,0,1:T(8,128)(2,1)}), bf16[2,4,128,4096]{3,2,0,1:T(8,128)(2,1)}, u32[]{:S(2)}, u32[]{:S(2)}) async-start(bf16[2,4,128,4096]{3,2,0,1:T(8,128)(2,1)} %copy.20), calls=%async_computation.3 | async-start | bytes 16777216 | tf_op jit(solution)/shard_map/all_to_all | solution.py:73
  1205.0 13.6 %copy-start.3 = (bf16[256,4096]{1,0:T(8,128)(2,1)S(1)}, bf16[256,4096]{1,0:T(8,128)(2,1)}, u32[]{:S(2)}) copy-start(bf16[256,4096]{1,0:T(8,128)(2,1)} %copy-done.2) | copy-start | bytes 6291460
Sparse Core Ops, SparseCore 0:
  17.1 141.9 all-gather.12
  160.6 139.2 all-gather.14
  301.5 139.2 all-gather.16
  442.2 139.2 all-gather.18
  582.9 139.2 all-gather.20
  723.5 139.2 all-gather.22
where the time goes:
time: 1230 us
  waiting for transfers between devices  490 us (40%)
  blocking collectives  383 us (31%)
  local copies, waits for them, and re-layouts  170 us (14%)
  matrix products  122 us (10%)
  other arithmetic  37 us (3%)
  between operations  14.4 us (1%)
    all_to_all x2, blocking collectives, device_step(): recv_buf = lax.all_to_all(send_buf, 'ep', 1, 1, tiled=True)  383 us
    all_to_all x2, waiting for transfers between devices, device_step(): lax.all_to_all(expert_out.reshape(n_local, owners, capacity, d_model), 'e...  350 us
    all_gather x2, waiting for transfers between devices, device_step(): down_full = lax.all_gather(down_w[layer_idx], 'fsdp', axis=1, tiled=True)  121 us
    dot_general x2, matrix products, expert_ffn(): jnp.einsum('erf,efd->erd', inner_act, down_full, preferred_element_type=j...  41.9 us
    dot_general x2, matrix products, expert_ffn(): jnp.einsum('erd,edf->erf', expert_rows, up_full, preferred_element_type=j...  40 us
    dot_general x2, matrix products, expert_ffn(): jnp.einsum('erd,edf->erf', expert_rows, gate_full, preferred_element_type...  38.5 us
    reduce_sum x2, other arithmetic, combine(): jnp.sum(gate_probs[..., None] * pair_out.astype(jnp.float32), axis=-2)  27.1 us
    gather x2, local copies, waits for them, and re-layouts, device_step(): back_buf.reshape(experts * capacity, d_model)[pair_slot]  26.1 us
  transfers between devices with their start and end apart: 8, of which 4 were waited for; matrix products, arithmetic and copies ran while one was open for 20% of the time, Pallas kernels for 0%

commit v1 on v0

v1 whole, which is shorter than its diff:
```python
import functools

import jax
import jax.numpy as jnp
from jax import lax
from jax.experimental import pallas as pl
from jax.experimental.pallas import tpu as pltpu
from jax.sharding import PartitionSpec as P

NORM_EPS = 1e-5
MESH = pl.DeviceIdType.MESH
ANY = pl.BlockSpec(memory_space=pl.ANY)
VMEM = pl.BlockSpec(memory_space=pltpu.VMEM)
VMEM_BYTES = 67_043_328
MATS = 3


def dot_nt(rows, weight_t):
    return lax.dot_general(rows, weight_t, (((1,), (1,)), ((), ())), preferred_element_type=jnp.float32)


def dot(a, b):
    return jnp.dot(a, b, preferred_element_type=jnp.float32)


def layers_kernel(x_ref, norm_ref, router_ref, routes_ref, routes_row_ref, wg_ref, wu_ref, wd_ref,
                  y_ref, mate_w, far_w, mate_far_w,
                  hbuf, ranks, back, outb, picked, act, wgu, wdn, gates_ref, slots_ref,
                  ysend, yrecv, xsend, xrecv, msend, mrecv, fsend, frecv,
                  hsend, hrecv, tsend, trecv, rsend, rrecv, gu_sem, d_sem):
    n_layers, n_local, ff, width = wg_ref.shape
    tok = x_ref.shape[0]
    experts = router_ref.shape[1]
    cap = back.shape[1]
    n_ep = hbuf.shape[1]
    chunk = wdn.shape[3]
    chunks = width // chunk
    half = width // 2
    weights = (wg_ref, wu_ref, wd_ref)
    pieces = n_local * MATS
    ep = lax.axis_index("ep")
    fs = lax.axis_index("fsdp")
    rep = lax.axis_index("rep")

    def xor(i, bits):
        out = i
        for b in (1, 2):
            if bits & b:
                out = out + b - 2 * b * ((i // b) % 2)
        return out

    far_id, mate_id, rep_id = {"fsdp": xor(fs, 2)}, {"fsdp": xor(fs, 1)}, {"rep": 1 - rep}
    barrier = pltpu.get_barrier_semaphore()
    peers = [far_id, mate_id, rep_id] + [{"ep": xor(ep, q)} for q in range(1, n_ep)]
    for peer in peers:
        pl.semaphore_signal(barrier, inc=1, device_id=peer, device_id_type=MESH)
    pl.semaphore_wait(barrier, len(peers))

    def remote(src, dst, send, recv, device):
        return pltpu.make_async_remote_copy(src_ref=src, dst_ref=dst, send_sem=send, recv_sem=recv, device_id=device, device_id_type=MESH)

    mine = pl.ds(pl.multiple_of(rep * half, half), half)
    other = pl.ds(pl.multiple_of((1 - rep) * half, half), half)

    def split(i):
        return i // pieces, (i % pieces) // MATS, weights[i % MATS]

    def y_copy(i):
        l, k, w = split(i)
        return remote(w.at[l, k, :, mine], far_w.at[i, :, mine], ysend.at[i], yrecv.at[i], far_id)

    def x_copy(i):
        return remote(far_w.at[i, :, mine], far_w.at[i, :, mine], xsend.at[i], xrecv.at[i], rep_id)

    def x_arrival(i):
        return remote(far_w.at[i, :, other], far_w.at[i, :, other], xsend.at[i], xrecv.at[i], rep_id)

    def m_copy(i):
        l, k, w = split(i)
        return remote(w.at[l, k], mate_w.at[i], msend.at[i], mrecv.at[i], mate_id)

    def f_copy(i):
        return remote(far_w.at[i], mate_far_w.at[i], fsend.at[i], frecv.at[i], mate_id)

    def pass_x(i):
        y_copy(i).wait_recv()
        x_copy(i).start()

    def pass_mate(i):
        x_arrival(i).wait_recv()
        f_copy(i).start()

    def weights_ready(i):
        m_copy(i).wait_recv()
        f_copy(i).wait_recv()

    def hop_copy(l, s, up):
        block = ep - s + 1 if up else ep + s - 1
        block = jnp.clip(block, 0, n_ep - 1)
        to = jnp.clip(ep + 1 if up else ep - 1, 0, n_ep - 1)
        d = 0 if up else 1
        data = remote(hbuf.at[l, block], hbuf.at[l, block], hsend.at[l, d, s - 1], hrecv.at[l, d, s - 1], {"ep": to})
        if l:
            return (data,)
        return data, remote(ranks.at[block], ranks.at[block], tsend.at[d, s - 1], trecv.at[d, s - 1], {"ep": to})

    def sends(s, up):
        return jnp.logical_and(ep >= s - 1, ep < n_ep - 1) if up else jnp.logical_and(ep <= n_ep - s, ep > 0)

    def arrives(s, up):
        return ep >= s if up else ep < n_ep - s

    def hop_start(l, s):
        for up in (True, False):
            @pl.when(sends(s, up))
            def _(up=up):
                for copy in hop_copy(l, s, up):
                    copy.start()

    def hop_wait(l, s):
        for up in (True, False):
            @pl.when(arrives(s, up))
            def _(up=up):
                for copy in hop_copy(l, s, up):
                    copy.wait_recv()

    def hop_drain(l):
        for s in range(1, n_ep):
            for up in (True, False):
                @pl.when(sends(s, up))
                def _(s=s, up=up):
                    for copy in hop_copy(l, s, up):
                        copy.wait_send()

    def routing():
        a = lax.broadcasted_iota(jnp.int32, (tok, tok), 0)
        b = lax.broadcasted_iota(jnp.int32, (tok, tok), 1)
        upper = (a < b).astype(jnp.float32).astype(jnp.bfloat16)
        lower = (a > b).astype(jnp.float32).astype(jnp.bfloat16)
        for l in range(n_layers):
            ids = lax.broadcasted_iota(jnp.int32, (experts, tok), 0)
            chosen = jnp.logical_or(ids == routes_row_ref[l, 0:1, :], ids == routes_row_ref[l, 1:2, :])
            rank = dot(chosen.astype(jnp.float32).astype(jnp.bfloat16), upper)
            ranks[ep, pl.ds(l * experts, experts), :] = jnp.where(chosen, rank, -1.0)
            ids = lax.broadcasted_iota(jnp.int32, (tok, experts), 1)
            choice = [routes_ref[l, :, j:j + 1] for j in range(2)]
            chosen = jnp.logical_or(ids == choice[0], ids == choice[1])
            rank = dot(lower, chosen.astype(jnp.float32).astype(jnp.bfloat16))
            for j in range(2):
                pair_rank = jnp.sum(jnp.where(ids == choice[j], rank, 0.0), axis=1, keepdims=True).astype(jnp.int32)
                slots_ref[l, :, j:j + 1] = ((choice[j] // n_local) ^ ep) * (n_local * cap) + (choice[j] % n_local) * cap + pair_rank

    def norm(src_ref, l):
        h_ref = hbuf.at[l, ep]

        def cols_of(c):
            return pl.ds(pl.multiple_of(c * chunk, chunk), chunk)

        def sq_step(c, sq):
            y = src_ref[:, cols_of(c)].astype(jnp.float32)
            return sq + jnp.sum(y * y, axis=1, keepdims=True)

        inv = lax.rsqrt(lax.fori_loop(0, chunks, sq_step, jnp.zeros((tok, 1), jnp.float32)) / width + NORM_EPS)

        def h_step(c, _):
            cols = cols_of(c)
            h_ref[:, cols] = (src_ref[:, cols].astype(jnp.float32) * inv * norm_ref[l:l + 1, cols]).astype(jnp.bfloat16)
            return _

        lax.fori_loop(0, chunks, h_step, 0)

    def gates(l):
        logits = dot_nt(hbuf[l, ep], router_ref[l])
        ids = lax.broadcasted_iota(jnp.int32, logits.shape, 1)
        p = [jnp.sum(jnp.where(ids == routes_ref[l, :, j:j + 1], logits, 0.0), axis=1, keepdims=True) for j in range(2)]
        top = jnp.maximum(p[0], p[1])
        e = [jnp.exp(p[j] - top) for j in range(2)]
        for j in range(2):
            gates_ref[:, j:j + 1] = e[j] / (e[0] + e[1])

    def ffn(l, k, qs):
        base = (l * n_local + k) * MATS
        rows = len(qs) * cap

        def source(f, m):
            return (weights[m].at[l, k], mate_w.at[base + m], far_w.at[base + m], mate_far_w.at[base + m])[f]

        def gu_copies(f):
            return [pltpu.make_async_copy(source(f, m), wgu.at[f % 2, m], gu_sem.at[f % 2, m]) for m in range(2)]

        def d_copies(c, slot):
            cols = pl.ds(pl.multiple_of(c * chunk, chunk), chunk)
            return [pltpu.make_async_copy(source(f, 2).at[:, cols], wdn.at[slot, f], d_sem.at[slot, f]) for f in range(4)]

        for f in range(2):
            for copy in gu_copies(f):
                copy.start()
        for copy in d_copies(0, 0):
            copy.start()
        slot_ids = lax.broadcasted_iota(jnp.int32, (cap, tok), 0)
        for n, q in enumerate(qs):
            block = xor(ep, q)
            row = ranks[block, pl.ds(l * experts + ep * n_local + k, 1), :].astype(jnp.int32)
            pick = (slot_ids == row).astype(jnp.float32).astype(jnp.bfloat16)

            def pick_cols(c, _, n=n, block=block, pick=pick):
                cols = pl.ds(pl.multiple_of(c * chunk, chunk), chunk)
                picked[pl.ds(n * cap, cap), cols] = dot(pick, hbuf[l, block, :, cols]).astype(jnp.bfloat16)
                return _

            lax.fori_loop(0, chunks, pick_cols, 0)

        def up_step(f, _):
            slot = f % 2
            for m in range(2):
                pltpu.make_async_copy(weights[m].at[l, k], wgu.at[slot, m], gu_sem.at[slot, m]).wait()
            pre_gate = dot_nt(picked[pl.ds(0, rows), :], wgu[slot, 0])
            pre_up = dot_nt(picked[pl.ds(0, rows), :], wgu[slot, 1])
            act[f, pl.ds(0, rows), :] = (jax.nn.silu(pre_gate) * pre_up).astype(jnp.bfloat16)
            for g in range(2):
                @pl.when(f == g)
                def _(g=g):
                    for copy in gu_copies(g + 2):
                        copy.start()
            return 0

        lax.fori_loop(0, 4, up_step, 0)

        def down_step(c, _):
            slot = c % 2

            @pl.when(c + 1 < chunks)
            def _():
                for copy in d_copies(jnp.minimum(c + 1, chunks - 1), (c + 1) % 2):
                    copy.start()

            for copy in d_copies(c, slot):
                copy.wait()
            cols = pl.ds(pl.multiple_of(c * chunk, chunk), chunk)
            total = dot(act[0, pl.ds(0, rows), :], wdn[slot, 0])
            for f in range(1, 4):
                total += dot(act[f, pl.ds(0, rows), :], wdn[slot, f])
            out = total.astype(jnp.bfloat16)
            for n, q in enumerate(qs):
                piece = out[n * cap:(n + 1) * cap]
                if q == 0:
                    back[k, :, cols] = piece
                else:
                    outb[(q - 1) * n_local + k, :, cols] = piece
            return 0

        lax.fori_loop(0, chunks, down_step, 0)
        for q in qs:
            if q:
                return_copy(q, k).start()

    def return_copy(q, k):
        j = (q - 1) * n_local + k
        return remote(outb.at[j], back.at[q * n_local + k], rsend.at[j], rrecv.at[j], {"ep": xor(ep, q)})

    def combine(src_ref, l):
        for q in range(1, n_ep):
            for k in range(n_local):
                return_copy(q, k).wait_recv()
        total = n_ep * n_local * cap
        ids = lax.broadcasted_iota(jnp.int32, (tok, total), 1)
        pick = [(ids == slots_ref[l, :, j:j + 1]).astype(jnp.float32).astype(jnp.bfloat16) for j in range(2)]

        def step(c, _):
            cols = pl.ds(pl.multiple_of(c * chunk, chunk), chunk)
            rows = back[:, :, cols].reshape(total, chunk)
            mixed = gates_ref[:, 0:1] * dot(pick[0], rows) + gates_ref[:, 1:2] * dot(pick[1], rows)
            y_ref[:, cols] = (src_ref[:, cols].astype(jnp.float32) + mixed).astype(jnp.bfloat16)
            return _

        lax.fori_loop(0, chunks, step, 0)
        for q in range(1, n_ep):
            for k in range(n_local):
                return_copy(q, k).wait_send()

    for i in range(pieces):
        y_copy(i).start()
    routing()
    norm(x_ref, 0)
    hop_start(0, 1)
    for i in range(pieces):
        m_copy(i).start()
    gates(0)
    pass_x(0)
    hop_wait(0, 1)
    hop_start(0, 2)
    pass_x(1)
    pass_mate(0)
    pass_x(2)
    pass_mate(1)
    hop_wait(0, 2)
    hop_start(0, 3)
    pass_mate(2)
    pass_x(3)
    for i in range(MATS):
        weights_ready(i)
    ffn(0, 0, (2,))
    hop_wait(0, 3)
    pass_mate(3)
    ffn(0, 0, (3,))
    pass_x(4)
    pass_mate(4)
    for i in range(pieces, 2 * pieces):
        y_copy(i).start()
    ffn(0, 0, (0, 1))
    pass_x(5)
    pass_mate(5)
    for i in range(pieces, 2 * pieces):
        m_copy(i).start()
    for i in range(MATS, pieces):
        weights_ready(i)
    ffn(0, 1, (2,))
    pass_x(6)
    ffn(0, 1, (3,))
    pass_x(7)
    pass_mate(6)
    ffn(0, 1, (0, 1))
    pass_x(8)
    pass_mate(7)
    pass_x(9)
    pass_mate(8)
    combine(x_ref, 0)
    norm(y_ref, 1)
    hop_start(1, 1)
    gates(1)
    pass_x(10)
    pass_mate(9)
    pass_x(11)
    hop_wait(1, 1)
    hop_start(1, 2)
    for i in range(6, 9):
        weights_ready(i)
    ffn(1, 0, (0, 1))
    pass_mate(10)
    hop_wait(1, 2)
    hop_start(1, 3)
    ffn(1, 0, (2,))
    pass_mate(11)
    for i in range(9, 12):
        weights_ready(i)
    ffn(1, 1, (2,))
    hop_wait(1, 3)
    ffn(1, 0, (3,))
    ffn(1, 1, (3,))
    ffn(1, 1, (0, 1))
    combine(y_ref, 1)
    hop_drain(0)
    hop_drain(1)
    for i in range(2 * pieces):
        y_copy(i).wait_send()
        x_copy(i).wait_send()
        m_copy(i).wait_send()
        f_copy(i).wait_send()


def moe_layers(x, norm_w, router_t, routes, routes_row, wg, wu, wd, n_ep):
    n_layers, n_local, ff, width = wg.shape
    tok = x.shape[0]
    experts = router_t.shape[1]
    cap = tok // 2
    chunk = min(512, width // 2)
    n = n_layers * n_local * MATS
    bf = jnp.bfloat16
    dma = pltpu.SemaphoreType.DMA
    copies = jax.ShapeDtypeStruct((n, ff, width), bf)
    return pl.pallas_call(
        layers_kernel,
        out_shape=(jax.ShapeDtypeStruct((tok, width), bf), copies, copies, copies),
        in_specs=[VMEM] * 5 + [ANY] * 3, out_specs=(VMEM, ANY, ANY, ANY),
        scratch_shapes=[
            pltpu.VMEM((n_layers, n_ep, tok, width), bf), pltpu.VMEM((n_ep, n_layers * experts, tok), jnp.float32),
            pltpu.VMEM((n_ep * n_local, cap, width), bf), pltpu.VMEM(((n_ep - 1) * n_local, cap, width), bf),
            pltpu.VMEM((2 * cap, width), bf), pltpu.VMEM((4, 2 * cap, ff), bf),
            pltpu.VMEM((2, 2, ff, width), bf), pltpu.VMEM((2, 4, ff, chunk), bf),
            pltpu.VMEM((tok, 2), jnp.float32), pltpu.VMEM((n_layers, tok, 2), jnp.int32),
        ] + [dma((n,))] * 8 + [dma((n_layers, 2, n_ep - 1))] * 2 + [dma((2, n_ep - 1))] * 2
          + [dma(((n_ep - 1) * n_local,))] * 2 + [dma((2, 2)), dma((2, 4))],
        compiler_params=pltpu.CompilerParams(collective_id=0, has_side_effects=True, vmem_limit_bytes=VMEM_BYTES),
        name="moe_layers",
    )(x, norm_w, router_t, routes, routes_row, wg, wu, wd)[0]


def solution(mesh):
    token_spec = P(("rep", "ep", "fsdp"), None)
    expert_in_spec = P(None, "ep", None, "fsdp")
    expert_out_spec = P(None, "ep", "fsdp", None)
    route_spec = P(None, ("rep", "ep", "fsdp"), None)
    n_ep = mesh.shape["ep"]

    def device_step(x_in, norm_w, router_w, gate_w, up_w, down_w, routes):
        return moe_layers(x_in, norm_w, router_w.swapaxes(1, 2), routes, routes.swapaxes(1, 2),
                          gate_w.swapaxes(2, 3), up_w.swapaxes(2, 3), down_w, n_ep)

    return jax.shard_map(device_step, mesh=mesh,
                         in_specs=(token_spec, P(), P(), expert_in_spec, expert_in_spec, expert_out_spec, route_spec),
                         out_specs=token_spec, check_vma=False)
```

time: 1230 us -> 683 us (0.56)
  Pallas kernels: 0 us -> 666 us
  waiting for transfers between devices: 490 us -> 0 us
  blocking collectives: 383 us -> 0 us
  local copies, waits for them, and re-layouts: 170 us -> 4.67 us
  matrix products: 122 us -> 0 us
  other arithmetic: 37 us -> 0 us
  between operations: 14.4 us -> 0.01 us
    pallas_call x0 -> x1, Pallas kernels: none -> 666 us  [moe_layers(): pl.pallas_call(layers_kernel, out_shape=(jax.ShapeDtypeStruct((tok, width...]
    all_to_all x2 -> x0, blocking collectives: 383 us -> none  [device_step(): recv_buf = lax.all_to_all(send_buf, 'ep', 1, 1, tiled=True)]
    all_to_all x2 -> x0, waiting for transfers between devices: 350 us -> none  [device_step(): lax.all_to_all(expert_out.reshape(n_local, owners, capacity, d_model), 'e...]
    all_gather x6 -> x0, waiting for transfers between devices: 139 us -> none  [the longest x2 121 us: device_step(): down_full = lax.all_gather(down_w[layer_idx], 'fsdp', axis=1, tiled=True)]
    dot_general x8 -> x0, matrix products: 122 us -> none  [the longest x2 41.9 us: expert_ffn(): jnp.einsum('erf,efd->erd', inner_act, down_full, preferred_element_type=j...]
    gather x10 -> x0, local copies, waits for them, and re-layouts: 49.1 us -> none  [the longest x2 26.1 us: device_step(): back_buf.reshape(experts * capacity, d_model)[pair_slot]]
    slice x6 -> x0, local copies, waits for them, and re-layouts: 32 us -> none  [the longest x1 10.4 us: device_step(): up_full = lax.all_gather(up_w[layer_idx], 'fsdp', axis=2, tiled=True)]
    all_to_all x4 -> x0, local copies, waits for them, and re-layouts: 31 us -> none  [the longest x2 15.5 us: device_step(): lax.all_to_all(expert_out.reshape(n_local, owners, capacity, d_model), 'e...]
  transfers between devices with their start and end apart: 8 -> 0, of which waited for: 4 -> 0; matrix products, arithmetic and copies ran while one was open for 20% -> 0% of each run, Pallas kernels for 0% -> 0%
where the time goes in v1:
time: 683 us; the launch traced here: 671 us
  Pallas kernels  666 us (98%)
    pallas_call x1, Pallas kernels, moe_layers(): pl.pallas_call(layers_kernel, out_shape=(jax.ShapeDtypeStruct((tok, width...  666 us

profile of v1, /device:TPU:0, one launch (start us, length us, event | category | flops | bytes accessed | tf_op | source)
XLA Modules:
  0.0 670.6 jit_solution(16821038206419774008)
XLA Ops:
  0.0 1.5 copy.8.routes_ref
  1.5 665.9 %moe_layers.1 = (bf16[256,4096]{1,0:T(8,128)(2,1)}, bf16[12,344,4096]{2,1,0:T(8,128)(2,1)}, bf16[12,344,4096]{2,1,0:T(8,128)(2,1)}, bf16[12,344,4096]{2,1,0:T(8,128)(2,1)}) custom-call(bf16[256,4096]{1,0:T(8,128)(2,1)} %x_ref.1, f32[2,4096]{1,0:T(2,128)} %norm_ref.1, bf16[2,8,4096]{2,1,0:T(8,128)(2,1)} %bitcast.6, s32[2,256,2]{2,1,0:T(8,128)} %copy.8.routes_ref, ...), custom_call_target="tpu_custom_call" | custom-call | tf_op jit(solution)/shard_map/moe_layers/pallas_call | solution.py:371
  667.4 3.1 copy.10
